TPU v7x, 32 devices: a whole 2x2x4 slice. The times are simulated.
32 devices in a mesh: dp: 2 (over x), expert: 16 (over z, y, core).
Axes of the slice: x: 2, y: 2, z: 4, core: 2. Of those that a mesh axis runs over, the one named last changes fastest.
Arguments:
- cotangent: bfloat16 [4096, 3584], P(('dp', 'expert')), may hold values from -0.59765625 to 0.59765625
- expert_ids: int32 [4096, 1], P(('dp', 'expert')), may hold values from 0 to 3; in each aligned block of 128 rows (0 to 127, 128 to 255, ...) at most 48 rows name the same one
- route_weights: float32 [4096, 1], P(('dp', 'expert')), may hold values from 0.1 to 1
- gate_pre: bfloat16 [1536, 4096], P('dp', 'expert'), may hold values from -5 to 5
- up_pre: bfloat16 [1536, 4096], P('dp', 'expert'), may hold values from -5 to 5
- down_weight: bfloat16 [3584, 4096], P('dp', 'expert'), may hold values from -0.1875 to 0.1875
Outputs:
- weight_grad: bfloat16 [3584, 4096], P('dp', 'expert')
- gate_grad: bfloat16 [1536, 4096], P('dp', 'expert')
- up_grad: bfloat16 [1536, 4096], P('dp', 'expert')
Inputs may be any that keep to these rules, and one draw needn't show every extreme that they name: `expert_ids`: each token names one expert. Among the tokens of one device, at most 48 name the same expert, and in every draw some expert is named by exactly 48 tokens of some device.
All inputs are finite; a program needn't handle non-finite values.
Results may differ from a plain program's by a relative error of at most 0.013.
Values may be sent and summed in bfloat16 or wider, within the bound.
A program may use at most 64 MiB of HBM per device.

v0:
```python
import functools

import jax
import jax.numpy as jnp
from jax import lax
from jax.experimental import pallas as pl
from jax.experimental.pallas import tpu as pltpu
from jax.sharding import PartitionSpec as P

SPLIT = 4
EARLY = 2
BUILD = 3
LAG = 2


def kernel(
    sizes,
    cot_hbm,
    ids_hbm,
    weights_hbm,
    gate_hbm,
    up_hbm,
    down_hbm,
    wgrad_ref,
    ggrad_ref,
    ugrad_ref,
    cot_ref,
    ids_ref,
    weights_ref,
    gate_ref,
    up_ref,
    down_ref,
    load,
    sendbuf,
    routed,
    cot_in,
    ids_in,
    weights_in,
    up_out,
    up_in,
    upstream,
    slope,
    active,
    product,
    picker,
    scale,
    z_send,
    z_recv,
    y_send,
    y_recv,
    c_send,
    c_recv,
    x_send,
    x_recv,
    i_send,
    i_recv,
    p_send,
    p_recv,
    u_send,
    u_recv,
):
    n, experts, cap, chunks, width, aligned = sizes
    own = chunks // n
    away = chunks - own
    early = min(EARLY, own - 1)
    ahead = min(BUILD, chunks)
    tokens = ids_ref.shape[1]
    dp = lax.axis_index("dp")
    me = lax.axis_index("expert")
    e, lane = me // SPLIT, me % SPLIT
    across = me - lane + (lane + 2) % SPLIT
    beside = me - lane + (lane // 2) * 2 + (lane + 1) % 2
    lane_across = (lane + 2) % SPLIT

    loads = [
        pltpu.make_async_copy(source, to, load.at[i])
        for i, (source, to) in enumerate(
            (
                (cot_hbm, cot_ref),
                (gate_hbm, gate_ref),
                (up_hbm, up_ref),
                (down_hbm, down_ref),
                (ids_hbm, ids_ref),
                (weights_hbm, weights_ref),
            )
        )
    ]
    for i in (4, 5, 0, 1, 2, 3):
        loads[i].start()

    barrier = pltpu.get_barrier_semaphore()

    def greet(target):
        pl.semaphore_signal(
            barrier, inc=1, device_id=target, device_id_type=pl.DeviceIdType.MESH
        )

    for k in range(1, experts):
        greet({"expert": (e + k) % experts * SPLIT + lane})
    greet({"expert": across})
    greet({"expert": beside})
    for k in range(1, n):
        greet({"dp": (dp + k) % n})

    def send(source, to, sent, arrived, device):
        return pltpu.make_async_remote_copy(
            src_ref=source,
            dst_ref=to,
            send_sem=sent,
            recv_sem=arrived,
            device_id=device,
            device_id_type=pl.DeviceIdType.MESH,
        )

    def chunk_at(t):
        late = jnp.where(t < early + away, own - early, -away)
        return t + jnp.where(t < early, 0, late)

    def columns_of(share, j):
        if aligned:
            return cot_ref.at[:, pl.ds(pl.multiple_of((share * own + j) * width, 128), width)]
        return cot_ref.at[share * own + j]

    def cot_copy(i):
        to = (dp - 1 - i // own + n) % n
        return send(columns_of(to, i % own), cot_in.at[i], x_send.at[i], x_recv.at[i], {"dp": to})

    def ids_copy(k):
        return send(
            ids_ref, ids_in.at[k - 1], i_send.at[k - 1, 0], i_recv.at[k - 1, 0], {"dp": (dp - k + n) % n}
        )

    def weights_copy(k):
        return send(
            weights_ref, weights_in.at[k - 1], i_send.at[k - 1, 1], i_recv.at[k - 1, 1], {"dp": (dp - k + n) % n}
        )

    def product_copy(k):
        return send(
            product.at[0], product.at[k], p_send.at[k - 1], p_recv.at[k - 1], {"dp": (dp - k + n) % n}
        )

    def up_copy(i):
        return send(up_out.at[i], up_in.at[i], u_send.at[i], u_recv.at[i], {"dp": (dp + 1 + i) % n})

    def pick(k, ids_row, weight_row):
        shape = (tokens, tokens)
        first = lax.broadcasted_iota(jnp.int32, shape, 0)
        second = lax.broadcasted_iota(jnp.int32, shape, 1)
        names = lax.broadcasted_iota(jnp.int32, (-(-experts // 16) * 16, tokens), 0) == ids_row
        before = jnp.where(first < second, 1.0, 0.0).astype(jnp.bfloat16)
        earlier = jnp.dot(
            jnp.where(names, 1.0, 0.0).astype(jnp.bfloat16), before, preferred_element_type=jnp.float32
        )
        position = jnp.sum(jnp.where(names, earlier, 0.0), axis=0, keepdims=True).astype(jnp.int32)
        target = ids_row * cap + position
        chosen = lax.broadcasted_iota(jnp.int32, (experts * cap, tokens), 0) == target
        picker[k] = jnp.where(chosen, 1.0, 0.0).astype(jnp.bfloat16)
        scale[k] = jnp.sum(jnp.where(chosen, weight_row, 0.0), axis=1, keepdims=True)

    def place(q, k, columns):
        picked = jnp.dot(picker[k], columns, preferred_element_type=jnp.float32)
        rows = (picked * scale[k]).astype(jnp.bfloat16).reshape(experts, cap, width)
        sendbuf[q] = rows
        routed[q, e, lane] = sendbuf[q, e]

    def build(t):
        q = chunk_at(t)

        @pl.when(q < own)
        def _():
            place(q, 0, columns_of(dp, q)[...])

        @pl.when(q >= own)
        def _():
            cot_copy(q - own).wait_recv()
            place(q, q // own, cot_in[q - own])

    def from_source(q, source):
        at = routed.at[q, source, lane]
        return send(at, at, y_send.at[q], y_recv.at[q], {"expert": across})

    def to_expert(t):
        q = chunk_at(t)
        for k in range(1, experts):
            there = (e + k) % experts
            send(
                sendbuf.at[q, there],
                routed.at[q, e, lane],
                z_send.at[q],
                z_recv.at[q],
                {"expert": there * SPLIT + lane},
            ).start()
        from_source(q, e).start()

    def over_y(q):
        at = routed.at[q, :, lane]
        return send(at, at, y_send.at[q], y_recv.at[q], {"expert": across})

    def over_core(q, turn):
        at = routed.at[q, :, lane if turn == 0 else lane_across]
        return send(at, at, c_send.at[q, turn], c_recv.at[q, turn], {"expert": beside})

    def all_but_one(ref_at, sem):
        pltpu.make_async_copy(ref_at, ref_at, sem).wait()

    loads[4].wait()
    loads[5].wait()
    pick(0, ids_ref[...], weights_ref[...])
    loads[0].wait()
    for j in range(early):
        place(j, 0, columns_of(dp, j)[...])
    pl.semaphore_wait(barrier, experts - 1 + 2 + n - 1)
    for k in range(1, n):
        ids_copy(k).start()
        weights_copy(k).start()

    @pl.loop(0, away)
    def _(i):
        cot_copy(i).start()

    for j in range(early):
        to_expert(j)

    rows_all = gate_ref.shape[0]
    piece = rows_all // 8
    loads[1].wait()
    loads[2].wait()

    @pl.loop(0, 8)
    def _(i):
        at = pl.ds(pl.multiple_of(i * piece, 16), piece)
        gate = gate_ref[at, :].astype(jnp.float32)
        up = up_ref[at, :].astype(jnp.float32)
        sig = jax.nn.sigmoid(gate)
        act = gate * sig
        active[at, :] = act
        slope[at, :] = up * sig * (1.0 + gate * (1.0 - sig))
        product[0, at, :] = (act * up).astype(jnp.bfloat16)
        for k in range(n):
            upstream[k, at, :] = jnp.zeros_like(act)

    for k in range(1, n):
        ids_copy(k).wait_recv()
        weights_copy(k).wait_recv()
        pick(k, ids_in[k - 1], weights_in[k - 1])
    for t in range(early, ahead):
        build(t)
    for t in range(early, ahead - 1):
        to_expert(t)
    for k in range(1, n):
        product_copy(k).start()
    loads[3].wait()

    def gradient(j):
        total = jnp.zeros((width, product.shape[2]), jnp.float32)
        for k in range(n):
            rows = routed[k * own + j].reshape(rows_all, width)
            total = total + lax.dot_general(
                rows, product[k], (((0,), (0,)), ((), ())), preferred_element_type=jnp.float32
            )
        wgrad_ref[j] = total.astype(jnp.bfloat16)

    @pl.loop(0, chunks + LAG + 1)
    def _(t):
        @pl.when(t + ahead < chunks)
        def _():
            build(t + ahead)

        @pl.when(t + ahead - 1 < chunks)
        def _():
            to_expert(t + ahead - 1)

        @pl.when(t < chunks)
        def _():
            q = chunk_at(t)
            all_but_one(routed.at[q, pl.ds(0, experts - 1), 0], z_recv.at[q])
            for k in range(1, experts):
                from_source(q, (e + k) % experts).start()
            over_core(q, 0).start()

        @pl.when((t >= LAG) & (t < chunks + LAG))
        def _():
            q = chunk_at(t - LAG)
            over_y(q).wait_recv()
            over_core(q, 1).start()

        @pl.when(t >= LAG + 1)
        def _():
            turn = t - LAG - 1
            q = chunk_at(turn)
            k, j = q // own, q % own
            over_core(q, 0).wait_recv()
            over_core(q, 1).wait_recv()
            rows = routed[q].reshape(rows_all, width)
            upstream[k] += jnp.dot(rows, down_ref[j], preferred_element_type=jnp.float32)

            @pl.when((k >= 1) & (j == own - 1))
            def _():
                up_out[k - 1] = upstream[k].astype(jnp.bfloat16)

            @pl.when(turn == early + away)
            def _():
                for i in range(1, n):
                    product_copy(i).wait_recv()
                for i in range(early):
                    gradient(i)

            @pl.when(turn >= early + away)
            def _():
                gradient(j)

            @pl.when((k >= 1) & (j == own - 1))
            def _():
                up_copy(k - 1).start()

    for k in range(1, n):
        up_copy(k - 1).wait_recv()

    @pl.loop(0, 8)
    def _(i):
        at = pl.ds(pl.multiple_of(i * piece, 16), piece)
        total = upstream[0, at, :]
        for k in range(1, n):
            total = total + up_in[k - 1, at, :].astype(jnp.float32)
        ggrad_ref[at, :] = (total * slope[at, :]).astype(jnp.bfloat16)
        ugrad_ref[at, :] = (total * active[at, :]).astype(jnp.bfloat16)

    @pl.loop(0, chunks)
    def _(q):
        all_but_one(sendbuf.at[q, pl.ds(0, experts - 1)], z_send.at[q])
        over_y(q).wait_send()
        over_core(q, 0).wait_send()
        over_core(q, 1).wait_send()

    @pl.loop(0, away)
    def _(i):
        cot_copy(i).wait_send()

    for k in range(1, n):
        ids_copy(k).wait_send()
        weights_copy(k).wait_send()
        product_copy(k).wait_send()
        up_copy(k - 1).wait_send()


def chunk_width(depth):
    for width in (256, 128):
        if depth % width == 0:
            return width, True
    return depth, False


def per_device(cotangent, expert_ids, route_weights, gate_pre, up_pre, down_weight):
    n = lax.axis_size("dp")
    devices = lax.axis_size("expert")
    experts = devices // SPLIT
    rows, hidden = gate_pre.shape
    capacity = rows // devices
    cap = -(-capacity // 16) * 16
    depth = down_weight.shape[0]
    width, aligned = chunk_width(depth)
    own = depth // width
    chunks = n * own
    away = chunks - own
    if not aligned:
        cotangent = cotangent.reshape(-1, chunks, width).swapaxes(0, 1)

    def widen(a):
        if cap == capacity:
            return a
        a = a.reshape(devices, capacity, hidden)
        return jnp.pad(a, ((0, 0), (0, cap - capacity), (0, 0))).reshape(devices * cap, hidden)

    def narrow(a):
        if cap == capacity:
            return a
        return a.reshape(devices, cap, hidden)[:, :capacity].reshape(rows, hidden)

    padded = devices * cap
    tokens = expert_ids.shape[0]
    half, full = jnp.bfloat16, jnp.float32
    vmem = pl.BlockSpec(memory_space=pltpu.VMEM)
    anywhere = pl.BlockSpec(memory_space=pltpu.HBM)
    dma = pltpu.SemaphoreType.DMA
    weight_grad, gate_grad, up_grad = pl.pallas_call(
        functools.partial(kernel, (n, experts, cap, chunks, width, aligned)),
        out_shape=(
            pltpu.VMEM((own, width, hidden), half),
            pltpu.VMEM((padded, hidden), half),
            pltpu.VMEM((padded, hidden), half),
        ),
        in_specs=[anywhere] * 6,
        out_specs=(vmem, vmem, vmem),
        scratch_shapes=[
            pltpu.VMEM(cotangent.shape, half),
            pltpu.VMEM((1, tokens), jnp.int32),
            pltpu.VMEM((1, tokens), full),
            pltpu.VMEM((padded, hidden), half),
            pltpu.VMEM((padded, hidden), half),
            pltpu.VMEM((own, width, hidden), half),
            dma((6,)),
            pltpu.VMEM((chunks, experts, cap, width), half),
            pltpu.VMEM((chunks, experts, SPLIT, cap, width), half),
            pltpu.VMEM((away, tokens, width), half),
            pltpu.VMEM((n - 1, 1, tokens), jnp.int32),
            pltpu.VMEM((n - 1, 1, tokens), full),
            pltpu.VMEM((n - 1, padded, hidden), half),
            pltpu.VMEM((n - 1, padded, hidden), half),
            pltpu.VMEM((n, padded, hidden), full),
            pltpu.VMEM((padded, hidden), full),
            pltpu.VMEM((padded, hidden), full),
            pltpu.VMEM((n, padded, hidden), half),
            pltpu.VMEM((n, experts * cap, tokens), half),
            pltpu.VMEM((n, experts * cap, 1), full),
            dma((chunks,)),
            dma((chunks,)),
            dma((chunks,)),
            dma((chunks,)),
            dma((chunks, 2)),
            dma((chunks, 2)),
            dma((away,)),
            dma((away,)),
            dma((n - 1, 2)),
            dma((n - 1, 2)),
            dma((n - 1,)),
            dma((n - 1,)),
            dma((n - 1,)),
            dma((n - 1,)),
        ],
        compiler_params=pltpu.CompilerParams(collective_id=0, has_side_effects=True),
    )(
        cotangent,
        expert_ids.reshape(1, -1),
        route_weights.reshape(1, -1),
        widen(gate_pre),
        widen(up_pre),
        down_weight.reshape(own, width, hidden),
    )
    return weight_grad.reshape(depth, hidden), narrow(gate_grad), narrow(up_grad)


def solution(mesh):
    placed = (
        P(("dp", "expert"), None),
        P(("dp", "expert"), None),
        P(("dp", "expert"), None),
        P("dp", "expert"),
        P("dp", "expert"),
        P("dp", "expert"),
    )
    return jax.shard_map(
        per_device,
        mesh=mesh,
        in_specs=placed,
        out_specs=(P("dp", "expert"), P("dp", "expert"), P("dp", "expert")),
        check_vma=False,
    )
```

profile of v0, /device:TPU:0, one launch (start us, length us, event | category | flops | bytes accessed | tf_op | source)
XLA Modules:
  0.0 48.0 jit_solution(4148448631675846605)
XLA Ops:
  0.6 45.0 %shard_map.85 = (bf16[7,256,256]{2,1,0:T(8,128)(2,1)S(1)}, bf16[768,256]{1,0:T(8,128)(2,1)S(1)}, bf16[768,256]{1,0:T(8,128)(2,1)S(1)}) custom-call(bf16[128,3584]{1,0:T(8,128)(2,1)} %cot_hbm.1, s32[1,128]{1,0:T(1,128)} %bitcast.6, f32[1,128]{1,0:T(1,128)} %bitcast.7, bf16[768,256]{1,0:T(8,128)(2,1)} %gate_hbm.1, bf16[768,256]{1,0:T(8,128)(2,1)} %up_hbm.1, ...), custom_call_target="tpu_custom_call" | custom-call | tf_op jit(solution)/shard_map/pallas_call | solution.py:386
  45.6 0.9 %copy.12 = bf16[1792,256]{1,0:T(8,128)(2,1)} copy(bf16[1792,256]{1,0:T(8,128)(2,1)S(1)} %bitcast.4) | data formatting | bytes 1835008
  46.5 0.7 %copy.13 = bf16[768,256]{1,0:T(8,128)(2,1)} copy(bf16[768,256]{1,0:T(8,128)(2,1)S(1)} %get-tuple-element.10) | data formatting | bytes 786432
  47.3 0.7 %copy.14 = bf16[768,256]{1,0:T(8,128)(2,1)} copy(bf16[768,256]{1,0:T(8,128)(2,1)S(1)} %get-tuple-element.11) | data formatting | bytes 786432
where the time goes:
time: 48.2 us; the launch traced here: 48 us
  Pallas kernels  45 us (93%)
  local copies, waits for them, and re-layouts  2.42 us (5%)
  between operations  0.64 us (1%)
    pallas_call x1, Pallas kernels, per_device(): pl.pallas_call(functools.partial(kernel, (n, experts, cap, chunks, width,...  45 us
    unnamed x3, local copies, waits for them, and re-layouts  2.42 us

commit v1 on v0

--- a/solution.py
+++ b/solution.py
@@ -123,7 +123,7 @@
 
     def cot_copy(i):
         to = (dp - 1 - i // own + n) % n
-        return send(columns_of(to, i % own), cot_in.at[i], x_send.at[i], x_recv.at[i], {"dp": to})
+        return send(columns_of(to, i % own), cot_in.at[i], x_send.at[0], x_recv.at[i], {"dp": to})
 
     def ids_copy(k):
         return send(
@@ -178,7 +178,7 @@
 
     def from_source(q, source):
         at = routed.at[q, source, lane]
-        return send(at, at, y_send.at[q], y_recv.at[q], {"expert": across})
+        return send(at, at, y_send.at[0], y_recv.at[q], {"expert": across})
 
     def to_expert(t):
         q = chunk_at(t)
@@ -187,7 +187,7 @@
             send(
                 sendbuf.at[q, there],
                 routed.at[q, e, lane],
-                z_send.at[q],
+                z_send.at[0],
                 z_recv.at[q],
                 {"expert": there * SPLIT + lane},
             ).start()
@@ -195,13 +195,13 @@
 
     def over_y(q):
         at = routed.at[q, :, lane]
-        return send(at, at, y_send.at[q], y_recv.at[q], {"expert": across})
+        return send(at, at, y_send.at[0], y_recv.at[q], {"expert": across})
 
     def over_core(q, turn):
         at = routed.at[q, :, lane if turn == 0 else lane_across]
-        return send(at, at, c_send.at[q, turn], c_recv.at[q, turn], {"expert": beside})
-
-    def all_but_one(ref_at, sem):
+        return send(at, at, c_send.at[0], c_recv.at[q], {"expert": beside})
+
+    def all_of(ref_at, sem):
         pltpu.make_async_copy(ref_at, ref_at, sem).wait()
 
     loads[4].wait()
@@ -274,7 +274,7 @@
         @pl.when(t < chunks)
         def _():
             q = chunk_at(t)
-            all_but_one(routed.at[q, pl.ds(0, experts - 1), 0], z_recv.at[q])
+            all_of(routed.at[q, pl.ds(0, experts - 1), 0], z_recv.at[q])
             for k in range(1, experts):
                 from_source(q, (e + k) % experts).start()
             over_core(q, 0).start()
@@ -290,8 +290,7 @@
             turn = t - LAG - 1
             q = chunk_at(turn)
             k, j = q // own, q % own
-            over_core(q, 0).wait_recv()
-            over_core(q, 1).wait_recv()
+            all_of(routed.at[q, :, pl.ds(0, 2)], c_recv.at[q])
             rows = routed[q].reshape(rows_all, width)
             upstream[k] += jnp.dot(rows, down_ref[j], preferred_element_type=jnp.float32)
 
@@ -326,22 +325,24 @@
         ggrad_ref[at, :] = (total * slope[at, :]).astype(jnp.bfloat16)
         ugrad_ref[at, :] = (total * active[at, :]).astype(jnp.bfloat16)
 
-    @pl.loop(0, chunks)
-    def _(q):
-        all_but_one(sendbuf.at[q, pl.ds(0, experts - 1)], z_send.at[q])
-        over_y(q).wait_send()
-        over_core(q, 0).wait_send()
-        over_core(q, 1).wait_send()
-
-    @pl.loop(0, away)
-    def _(i):
-        cot_copy(i).wait_send()
-
+    all_of(sendbuf.at[:, pl.ds(0, experts - 1)], z_send.at[0])
+    all_of(sendbuf, y_send.at[0])
+    all_of(routed.at[:, :, pl.ds(0, 2)], c_send.at[0])
+    all_of(cot_in, x_send.at[0])
     for k in range(1, n):
         ids_copy(k).wait_send()
         weights_copy(k).wait_send()
         product_copy(k).wait_send()
         up_copy(k - 1).wait_send()
+
+
+def store(*refs):
+    count = len(refs) // 2
+    copies = [pltpu.make_async_copy(refs[i], refs[count + i], refs[-1].at[i]) for i in range(count)]
+    for copy in copies:
+        copy.start()
+    for copy in copies:
+        copy.wait()
 
 
 def chunk_width(depth):
@@ -413,13 +414,13 @@
             pltpu.VMEM((n, padded, hidden), half),
             pltpu.VMEM((n, experts * cap, tokens), half),
             pltpu.VMEM((n, experts * cap, 1), full),
+            dma((1,)),
             dma((chunks,)),
+            dma((1,)),
             dma((chunks,)),
+            dma((1,)),
             dma((chunks,)),
-            dma((chunks,)),
-            dma((chunks, 2)),
-            dma((chunks, 2)),
-            dma((away,)),
+            dma((1,)),
             dma((away,)),
             dma((n - 1, 2)),
             dma((n - 1, 2)),
@@ -437,7 +438,16 @@
         widen(up_pre),
         down_weight.reshape(own, width, hidden),
     )
-    return weight_grad.reshape(depth, hidden), narrow(gate_grad), narrow(up_grad)
+    results = (weight_grad.reshape(depth, hidden), gate_grad, up_grad)
+    weight_grad, gate_grad, up_grad = pl.pallas_call(
+        store,
+        out_shape=[jax.ShapeDtypeStruct(a.shape, a.dtype) for a in results],
+        in_specs=[vmem] * len(results),
+        out_specs=[anywhere] * len(results),
+        scratch_shapes=[dma((len(results),))],
+        compiler_params=pltpu.CompilerParams(vmem_limit_bytes=1 << 22),
+    )(*results)
+    return weight_grad, narrow(gate_grad), narrow(up_grad)
 
 
 def solution(mesh):

time: 48.2 us -> 46.1 us (0.956)
  local copies, waits for them, and re-layouts: 2.42 us -> 0 us
    unnamed x3 -> x0, local copies, waits for them, and re-layouts: 2.42 us -> none
    pallas_call x0 -> x1, Pallas kernels: none -> 1.21 us  [per_device(): pl.pallas_call(store, out_shape=[jax.ShapeDtypeStruct(a.shape, a.dtype) f...]
    pallas_call x1, Pallas kernels: 45 us -> 44.1 us  [per_device(): pl.pallas_call(functools.partial(kernel, (n, experts, cap, chunks, width,...]
where the time goes in v1:
time: 46.1 us; the launch traced here: 46 us
  Pallas kernels  45.3 us (98%)
  between operations  0.64 us (1%)
    pallas_call x1, Pallas kernels, per_device(): pl.pallas_call(functools.partial(kernel, (n, experts, cap, chunks, width,...  44.1 us
    pallas_call x1, Pallas kernels, per_device(): pl.pallas_call(store, out_shape=[jax.ShapeDtypeStruct(a.shape, a.dtype) f...  1.21 us

profile of v1, /device:TPU:0, one launch (start us, length us, event | category | flops | bytes accessed | tf_op | source)
XLA Modules:
  0.0 46.0 jit_solution(17827973841565637565)
XLA Ops:
  0.6 44.1 %shard_map.85 = (bf16[7,256,256]{2,1,0:T(8,128)(2,1)S(1)}, bf16[768,256]{1,0:T(8,128)(2,1)S(1)}, bf16[768,256]{1,0:T(8,128)(2,1)S(1)}) custom-call(bf16[128,3584]{1,0:T(8,128)(2,1)} %cot_hbm.1, s32[1,128]{1,0:T(1,128)} %bitcast.6, f32[1,128]{1,0:T(1,128)} %bitcast.7, bf16[768,256]{1,0:T(8,128)(2,1)} %gate_hbm.1, bf16[768,256]{1,0:T(8,128)(2,1)} %up_hbm.1, ...), custom_call_target="tpu_custom_call" | custom-call | tf_op jit(solution)/shard_map/pallas_call | solution.py:387
  44.8 1.2 %shard_map.86 = (bf16[1792,256]{1,0:T(8,128)(2,1)}, bf16[768,256]{1,0:T(8,128)(2,1)}, bf16[768,256]{1,0:T(8,128)(2,1)}) custom-call(bf16[1792,256]{1,0:T(8,128)(2,1)S(1)} %bitcast.4, bf16[768,256]{1,0:T(8,128)(2,1)S(1)} %get-tuple-element.7.refs_1_, bf16[768,256]{1,0:T(8,128)(2,1)S(1)} %get-tuple-element.8.refs_2_), custom_call_target="tpu_custom_call" | custom-call | tf_op jit(solution)/shard_map/pallas_call | solution.py:442

commit v2 on v1

--- a/solution.py
+++ b/solution.py
@@ -64,6 +64,11 @@
     away = chunks - own
     early = min(EARLY, own - 1)
     ahead = min(BUILD, chunks)
+    home_turn = max(0, early + away - ahead) + 1
+    block = SPLIT * cap
+    final = chunks - 1
+    rush = early + away + 1
+    steady = final + LAG
     tokens = ids_ref.shape[1]
     dp = lax.axis_index("dp")
     me = lax.axis_index("expert")
@@ -71,22 +76,47 @@
     across = me - lane + (lane + 2) % SPLIT
     beside = me - lane + (lane // 2) * 2 + (lane + 1) % 2
     lane_across = (lane + 2) % SPLIT
+    paired = experts & (experts - 1) == 0
+    steps = sorted(range(1, experts), key=lambda k: -(k.bit_length()))
+
+    def partner(k):
+        if not paired:
+            return (e + k) % experts
+        there = e
+        for bit in range(k.bit_length()):
+            if k >> bit & 1:
+                there = there + (1 << bit) - (2 << bit) * (e // (1 << bit) % 2)
+        return there
+
+    def origin(k):
+        return partner(k) if paired else (e + experts - k) % experts
+
+    def share_of(ref, share):
+        if aligned:
+            return ref.at[:, pl.ds(pl.multiple_of(share * own * width, 128), own * width)]
+        return ref.at[pl.ds(share * own, own)]
 
     loads = [
         pltpu.make_async_copy(source, to, load.at[i])
         for i, (source, to) in enumerate(
             (
-                (cot_hbm, cot_ref),
+                (ids_hbm, ids_ref),
+                (weights_hbm, weights_ref),
+                (share_of(cot_hbm, dp), share_of(cot_ref, dp)),
                 (gate_hbm, gate_ref),
                 (up_hbm, up_ref),
                 (down_hbm, down_ref),
-                (ids_hbm, ids_ref),
-                (weights_hbm, weights_ref),
             )
         )
     ]
-    for i in (4, 5, 0, 1, 2, 3):
-        loads[i].start()
+    others = [
+        pltpu.make_async_copy(
+            share_of(cot_hbm, (dp + k) % n), share_of(cot_ref, (dp + k) % n), load.at[5 + k]
+        )
+        for k in range(1, n)
+    ]
+    for copy in loads[:3] + others:
+        copy.start()
 
     barrier = pltpu.get_barrier_semaphore()
 
@@ -95,8 +125,8 @@
             barrier, inc=1, device_id=target, device_id_type=pl.DeviceIdType.MESH
         )
 
-    for k in range(1, experts):
-        greet({"expert": (e + k) % experts * SPLIT + lane})
+    for k in steps:
+        greet({"expert": partner(k) * SPLIT + lane})
     greet({"expert": across})
     greet({"expert": beside})
     for k in range(1, n):
@@ -140,8 +170,11 @@
             product.at[0], product.at[k], p_send.at[k - 1], p_recv.at[k - 1], {"dp": (dp - k + n) % n}
         )
 
-    def up_copy(i):
-        return send(up_out.at[i], up_in.at[i], u_send.at[i], u_recv.at[i], {"dp": (dp + 1 + i) % n})
+    def up_copy(i, plane):
+        at = pl.ds(pl.multiple_of(plane * block, 16), block)
+        return send(
+            up_out.at[i, at], up_in.at[i, at], u_send.at[i], u_recv.at[i], {"dp": (dp + 1 + i) % n}
+        )
 
     def pick(k, ids_row, weight_row):
         shape = (tokens, tokens)
@@ -167,65 +200,76 @@
     def build(t):
         q = chunk_at(t)
 
-        @pl.when(q < own)
-        def _():
-            place(q, 0, columns_of(dp, q)[...])
-
         @pl.when(q >= own)
         def _():
             cot_copy(q - own).wait_recv()
             place(q, q // own, cot_in[q - own])
 
-    def from_source(q, source):
-        at = routed.at[q, source, lane]
-        return send(at, at, y_send.at[0], y_recv.at[q], {"expert": across})
+    def to_across(q, plane, arrived):
+        at = routed.at[q, plane, lane]
+        send(at, at, y_send.at[0], arrived, {"expert": across}).start()
+
+    def to_beside(at, arrived):
+        send(at, at, c_send.at[0], arrived, {"expert": beside}).start()
+
+    def forward_across(q):
+        all_of(routed.at[q, pl.ds(0, experts - 1), 0], y_recv.at[q])
+        for k in steps:
+            to_beside(routed.at[q, origin(k), lane_across], c_recv.at[q])
+
+    def to_plane(source, to, k, arrived):
+        send(source, to, z_send.at[0], arrived, {"expert": partner(k) * SPLIT + lane}).start()
 
     def to_expert(t):
         q = chunk_at(t)
-        for k in range(1, experts):
-            there = (e + k) % experts
-            send(
-                sendbuf.at[q, there],
-                routed.at[q, e, lane],
-                z_send.at[0],
-                z_recv.at[q],
-                {"expert": there * SPLIT + lane},
-            ).start()
-        from_source(q, e).start()
-
-    def over_y(q):
-        at = routed.at[q, :, lane]
-        return send(at, at, y_send.at[0], y_recv.at[q], {"expert": across})
-
-    def over_core(q, turn):
-        at = routed.at[q, :, lane if turn == 0 else lane_across]
-        return send(at, at, c_send.at[0], c_recv.at[q], {"expert": beside})
+        for i, k in enumerate(steps):
+            arrived = z_recv.at[t + (jnp.where(t == final, i, 0) if i else 0)]
+            to_plane(sendbuf.at[q, partner(k)], routed.at[q, e, lane], k, arrived)
+
+        @pl.when(q >= own)
+        def _():
+            to_across(q, e, y_recv.at[chunks + 1])
 
     def all_of(ref_at, sem):
         pltpu.make_async_copy(ref_at, ref_at, sem).wait()
 
-    loads[4].wait()
-    loads[5].wait()
+    def forward(q, k):
+        plane = origin(k)
+        to_across(q, plane, y_recv.at[q])
+        to_beside(routed.at[q, plane, lane], c_recv.at[q])
+
+    loads[0].wait()
+    loads[1].wait()
     pick(0, ids_ref[...], weights_ref[...])
-    loads[0].wait()
+    loads[2].wait()
     for j in range(early):
         place(j, 0, columns_of(dp, j)[...])
     pl.semaphore_wait(barrier, experts - 1 + 2 + n - 1)
+    for j in range(early):
+        to_expert(j)
     for k in range(1, n):
         ids_copy(k).start()
         weights_copy(k).start()
+    for copy in others:
+        copy.wait()
 
     @pl.loop(0, away)
     def _(i):
         cot_copy(i).start()
 
+    for copy in loads[3:]:
+        copy.start()
     for j in range(early):
-        to_expert(j)
+        to_across(j, e, y_recv.at[chunks])
+
+    @pl.loop(early, own)
+    def _(j):
+        place(j, 0, columns_of(dp, j)[...])
 
     rows_all = gate_ref.shape[0]
     piece = rows_all // 8
-    loads[1].wait()
-    loads[2].wait()
+    loads[3].wait()
+    loads[4].wait()
 
     @pl.loop(0, 8)
     def _(i):
@@ -240,17 +284,23 @@
         for k in range(n):
             upstream[k, at, :] = jnp.zeros_like(act)
 
+    @pl.loop(early, own)
+    def _(j):
+        to_across(j, e, y_recv.at[chunks])
+
+    to_beside(routed.at[pl.ds(0, own), e, lane], c_recv.at[chunks])
+
     for k in range(1, n):
         ids_copy(k).wait_recv()
         weights_copy(k).wait_recv()
         pick(k, ids_in[k - 1], weights_in[k - 1])
     for t in range(early, ahead):
         build(t)
-    for t in range(early, ahead - 1):
-        to_expert(t)
     for k in range(1, n):
         product_copy(k).start()
-    loads[3].wait()
+    loads[5].wait()
+    for t in range(early, ahead):
+        to_expert(t)
 
     def gradient(j):
         total = jnp.zeros((width, product.shape[2]), jnp.float32)
@@ -261,60 +311,123 @@
             )
         wgrad_ref[j] = total.astype(jnp.bfloat16)
 
-    @pl.loop(0, chunks + LAG + 1)
+    def compute(turn):
+        q = chunk_at(turn)
+        k, j = q // own, q % own
+
+        @pl.when(turn == 0)
+        def _():
+            all_of(routed.at[pl.ds(0, own), 0, pl.ds(0, 2)], c_recv.at[chunks])
+
+        all_of(routed.at[q, pl.ds(0, experts - 1), pl.ds(0, 2)], c_recv.at[q])
+
+        @pl.when(k == 0)
+        def _():
+            rows = routed[q].reshape(rows_all, width)
+            upstream[0] += jnp.dot(rows, down_ref[j], preferred_element_type=jnp.float32)
+
+        @pl.when(k >= 1)
+        def _():
+            for step in steps:
+                plane = origin(step)
+                at = pl.ds(pl.multiple_of(plane * block, 16), block)
+                rows = routed[q, plane].reshape(block, width)
+                upstream[k, at, :] += jnp.dot(rows, down_ref[j], preferred_element_type=jnp.float32)
+
+                @pl.when(j == own - 1)
+                def _():
+                    up_out[k - 1, at, :] = upstream[k, at, :].astype(jnp.bfloat16)
+
+        @pl.when(turn >= early + away)
+        def _():
+            gradient(j)
+
+        @pl.when((k >= 1) & (j == own - 1))
+        def _():
+            for step in steps:
+                up_copy(k - 1, origin(step)).start()
+
+    def early_gradients():
+        for k in range(1, n):
+            product_copy(k).wait_recv()
+        for j in range(early):
+            gradient(j)
+
+    @pl.loop(0, steady)
     def _(t):
+        @pl.when(t >= LAG)
+        def _():
+            @pl.when(t == LAG)
+            def _():
+                all_of(routed.at[pl.ds(0, own), 0, 0], y_recv.at[chunks])
+                to_beside(routed.at[pl.ds(0, own), e, lane_across], c_recv.at[chunks])
+
+            forward_across(chunk_at(t - LAG))
+
+        @pl.when(t < final)
+        def _():
+            q = chunk_at(t)
+            all_of(routed.at[q, pl.ds(0, experts - 1), 0], z_recv.at[t])
+            for k in steps:
+                forward(q, k)
+
+        @pl.when(t == final)
+        def _():
+            for i, k in enumerate(steps):
+                all_of(routed.at[own - 1, 0, 0], z_recv.at[final + i])
+                forward(own - 1, k)
+
+        @pl.when(t + ahead < early + away)
+        def _():
+            build(t + ahead)
+
+        @pl.when(t == home_turn)
+        def _():
+            theirs = pl.ds(own, away)
+            to_beside(routed.at[theirs, e, lane], c_recv.at[chunks + 1])
+            all_of(routed.at[theirs, 0, 0], y_recv.at[chunks + 1])
+            to_beside(routed.at[theirs, e, lane_across], c_recv.at[chunks + 1])
+
+        @pl.when(t == home_turn + 1)
+        def _():
+            all_of(routed.at[pl.ds(own, away), 0, pl.ds(0, 2)], c_recv.at[chunks + 1])
+            at = pl.ds(pl.multiple_of(e * block, 16), block)
+            for k in range(1, n):
+                total = jnp.zeros((block, product.shape[2]), jnp.float32)
+                for j in range(own):
+                    rows = routed[k * own + j, e].reshape(block, width)
+                    total = total + jnp.dot(rows, down_ref[j], preferred_element_type=jnp.float32)
+                up_out[k - 1, at, :] = total.astype(jnp.bfloat16)
+
+        @pl.when(t == rush + 1)
+        def _():
+            early_gradients()
+
+        @pl.loop(t - LAG - 1 + jnp.where(t == rush + 1, 1, 0), t - LAG + jnp.where(t == rush, 1, 0))
+        def _(turn):
+            @pl.when(turn >= 0)
+            def _():
+                compute(turn)
+
+        @pl.when(t == home_turn + 1)
+        def _():
+            for k in range(1, n):
+                up_copy(k - 1, e).start()
+
         @pl.when(t + ahead < chunks)
         def _():
-            build(t + ahead)
-
-        @pl.when(t + ahead - 1 < chunks)
-        def _():
-            to_expert(t + ahead - 1)
-
-        @pl.when(t < chunks)
-        def _():
-            q = chunk_at(t)
-            all_of(routed.at[q, pl.ds(0, experts - 1), 0], z_recv.at[q])
-            for k in range(1, experts):
-                from_source(q, (e + k) % experts).start()
-            over_core(q, 0).start()
-
-        @pl.when((t >= LAG) & (t < chunks + LAG))
-        def _():
-            q = chunk_at(t - LAG)
-            over_y(q).wait_recv()
-            over_core(q, 1).start()
-
-        @pl.when(t >= LAG + 1)
-        def _():
-            turn = t - LAG - 1
-            q = chunk_at(turn)
-            k, j = q // own, q % own
-            all_of(routed.at[q, :, pl.ds(0, 2)], c_recv.at[q])
-            rows = routed[q].reshape(rows_all, width)
-            upstream[k] += jnp.dot(rows, down_ref[j], preferred_element_type=jnp.float32)
-
-            @pl.when((k >= 1) & (j == own - 1))
-            def _():
-                up_out[k - 1] = upstream[k].astype(jnp.bfloat16)
-
-            @pl.when(turn == early + away)
-            def _():
-                for i in range(1, n):
-                    product_copy(i).wait_recv()
-                for i in range(early):
-                    gradient(i)
-
-            @pl.when(turn >= early + away)
-            def _():
-                gradient(j)
-
-            @pl.when((k >= 1) & (j == own - 1))
-            def _():
-                up_copy(k - 1).start()
+            to_expert(t + ahead)
+
+    forward_across(own - 1)
+    if rush + 1 >= steady:
+        early_gradients()
+
+    @pl.loop(final if rush == steady - 1 else final - 1, chunks)
+    def _(turn):
+        compute(turn)
 
     for k in range(1, n):
-        up_copy(k - 1).wait_recv()
+        all_of(up_in.at[k - 1], u_recv.at[k - 1])
 
     @pl.loop(0, 8)
     def _(i):
@@ -333,7 +446,7 @@
         ids_copy(k).wait_send()
         weights_copy(k).wait_send()
         product_copy(k).wait_send()
-        up_copy(k - 1).wait_send()
+        all_of(up_out.at[k - 1], u_send.at[k - 1])
 
 
 def store(*refs):
@@ -400,7 +513,7 @@
             pltpu.VMEM((padded, hidden), half),
             pltpu.VMEM((padded, hidden), half),
             pltpu.VMEM((own, width, hidden), half),
-            dma((6,)),
+            dma((5 + n,)),
             pltpu.VMEM((chunks, experts, cap, width), half),
             pltpu.VMEM((chunks, experts, SPLIT, cap, width), half),
             pltpu.VMEM((away, tokens, width), half),
@@ -415,11 +528,11 @@
             pltpu.VMEM((n, experts * cap, tokens), half),
             pltpu.VMEM((n, experts * cap, 1), full),
             dma((1,)),
-            dma((chunks,)),
+            dma((chunks + experts - 2,)),
             dma((1,)),
-            dma((chunks,)),
+            dma((chunks + 2,)),
             dma((1,)),
-            dma((chunks,)),
+            dma((chunks + 2,)),
             dma((1,)),
             dma((away,)),
             dma((n - 1, 2)),

time: 46.1 us -> 44.5 us (0.965)
  Pallas kernels: 45.3 us -> 43.7 us
    pallas_call x1, Pallas kernels: 44.1 us -> 42.5 us  [per_device(): pl.pallas_call(functools.partial(kernel, (n, experts, cap, chunks, width,...]
where the time goes in v2:
time: 44.5 us; the launch traced here: 44.3 us
  Pallas kernels  43.7 us (98%)
  between operations  0.64 us (1%)
    pallas_call x1, Pallas kernels, per_device(): pl.pallas_call(functools.partial(kernel, (n, experts, cap, chunks, width,...  42.5 us
    pallas_call x1, Pallas kernels, per_device(): pl.pallas_call(store, out_shape=[jax.ShapeDtypeStruct(a.shape, a.dtype) f...  1.21 us

profile of v2, /device:TPU:0, one launch (start us, length us, event | category | flops | bytes accessed | tf_op | source)
XLA Modules:
  0.0 44.3 jit_solution(16758174878998160614)
XLA Ops:
  0.6 42.5 %shard_map.85 = (bf16[7,256,256]{2,1,0:T(8,128)(2,1)S(1)}, bf16[768,256]{1,0:T(8,128)(2,1)S(1)}, bf16[768,256]{1,0:T(8,128)(2,1)S(1)}) custom-call(bf16[128,3584]{1,0:T(8,128)(2,1)} %cot_hbm.1, s32[1,128]{1,0:T(1,128)} %bitcast.6, f32[1,128]{1,0:T(1,128)} %bitcast.7, bf16[768,256]{1,0:T(8,128)(2,1)} %gate_hbm.1, bf16[768,256]{1,0:T(8,128)(2,1)} %up_hbm.1, ...), custom_call_target="tpu_custom_call" | custom-call | tf_op jit(solution)/shard_map/pallas_call | solution.py:500
  43.1 1.2 %shard_map.86 = (bf16[1792,256]{1,0:T(8,128)(2,1)}, bf16[768,256]{1,0:T(8,128)(2,1)}, bf16[768,256]{1,0:T(8,128)(2,1)}) custom-call(bf16[1792,256]{1,0:T(8,128)(2,1)S(1)} %bitcast.4, bf16[768,256]{1,0:T(8,128)(2,1)S(1)} %get-tuple-element.7.refs_1_, bf16[768,256]{1,0:T(8,128)(2,1)S(1)} %get-tuple-element.8.refs_2_), custom_call_target="tpu_custom_call" | custom-call | tf_op jit(solution)/shard_map/pallas_call | solution.py:555

commit v3 on v2

--- a/solution.py
+++ b/solution.py
@@ -1,4 +1,5 @@
 import functools
+import math
 
 import jax
 import jax.numpy as jnp
@@ -11,6 +12,8 @@
 EARLY = 2
 BUILD = 3
 LAG = 2
+VMEM_BYTES = 66400000
+LAST_LIMIT = 12 << 20
 
 
 def kernel(
@@ -22,8 +25,13 @@
     up_hbm,
     down_hbm,
     wgrad_ref,
-    ggrad_ref,
-    ugrad_ref,
+    routed,
+    product,
+    upstream,
+    up_in,
+    slope,
+    active,
+    spare,
     cot_ref,
     ids_ref,
     weights_ref,
@@ -32,16 +40,10 @@
     down_ref,
     load,
     sendbuf,
-    routed,
     cot_in,
     ids_in,
     weights_in,
     up_out,
-    up_in,
-    upstream,
-    slope,
-    active,
-    product,
     picker,
     scale,
     z_send,
@@ -304,12 +306,7 @@
 
     def gradient(j):
         total = jnp.zeros((width, product.shape[2]), jnp.float32)
-        for k in range(n):
-            rows = routed[k * own + j].reshape(rows_all, width)
-            total = total + lax.dot_general(
-                rows, product[k], (((0,), (0,)), ((), ())), preferred_element_type=jnp.float32
-            )
-        wgrad_ref[j] = total.astype(jnp.bfloat16)
+        wgrad_ref[j] = down_gradient(routed, product, own, j, range(n), total).astype(jnp.bfloat16)
 
     def compute(turn):
         q = chunk_at(turn)
@@ -338,7 +335,7 @@
                 def _():
                     up_out[k - 1, at, :] = upstream[k, at, :].astype(jnp.bfloat16)
 
-        @pl.when(turn >= early + away)
+        @pl.when((turn >= early + away) & (turn < final))
         def _():
             gradient(j)
 
@@ -352,6 +349,8 @@
             product_copy(k).wait_recv()
         for j in range(early):
             gradient(j)
+        total = jnp.zeros((width, product.shape[2]), jnp.float32)
+        spare[...] = down_gradient(routed, product, own, own - 1, range(1, n), total)
 
     @pl.loop(0, steady)
     def _(t):
@@ -428,15 +427,6 @@
 
     for k in range(1, n):
         all_of(up_in.at[k - 1], u_recv.at[k - 1])
-
-    @pl.loop(0, 8)
-    def _(i):
-        at = pl.ds(pl.multiple_of(i * piece, 16), piece)
-        total = upstream[0, at, :]
-        for k in range(1, n):
-            total = total + up_in[k - 1, at, :].astype(jnp.float32)
-        ggrad_ref[at, :] = (total * slope[at, :]).astype(jnp.bfloat16)
-        ugrad_ref[at, :] = (total * active[at, :]).astype(jnp.bfloat16)
 
     all_of(sendbuf.at[:, pl.ds(0, experts - 1)], z_send.at[0])
     all_of(sendbuf, y_send.at[0])
@@ -449,11 +439,65 @@
         all_of(up_out.at[k - 1], u_send.at[k - 1])
 
 
-def store(*refs):
-    count = len(refs) // 2
-    copies = [pltpu.make_async_copy(refs[i], refs[count + i], refs[-1].at[i]) for i in range(count)]
-    for copy in copies:
-        copy.start()
+def down_gradient(routed, product, own, j, shares, total):
+    rows_all = product.shape[1]
+    width = routed.shape[-1]
+    for k in shares:
+        rows = routed[k * own + j].reshape(rows_all, width)
+        total = total + lax.dot_general(
+            rows, product[k], (((0,), (0,)), ((), ())), preferred_element_type=jnp.float32
+        )
+    return total
+
+
+def finish(
+    wgrad_ref,
+    routed,
+    product,
+    upstream,
+    up_in,
+    slope,
+    active,
+    spare,
+    wgrad_out,
+    ggrad_out,
+    ugrad_out,
+    wgrad_last,
+    ggrad_ref,
+    ugrad_ref,
+    stored,
+):
+    own = wgrad_ref.shape[0]
+    n, rows_all, _ = product.shape
+    piece = rows_all // 8
+    copies = [
+        pltpu.make_async_copy(source, to, stored.at[i])
+        for i, (source, to) in enumerate(
+            (
+                (ggrad_ref, ggrad_out),
+                (ugrad_ref, ugrad_out),
+                (wgrad_last, wgrad_out.at[own - 1]),
+            )
+        )
+    ]
+    if own > 1:
+        done = pl.ds(0, own - 1)
+        copies.append(pltpu.make_async_copy(wgrad_ref.at[done], wgrad_out.at[done], stored.at[3]))
+        copies[3].start()
+
+    @pl.loop(0, 8)
+    def _(i):
+        at = pl.ds(pl.multiple_of(i * piece, 16), piece)
+        total = upstream[0, at, :]
+        for k in range(1, n):
+            total = total + up_in[k - 1, at, :].astype(jnp.float32)
+        ggrad_ref[at, :] = (total * slope[at, :]).astype(jnp.bfloat16)
+        ugrad_ref[at, :] = (total * active[at, :]).astype(jnp.bfloat16)
+
+    copies[0].start()
+    copies[1].start()
+    wgrad_last[...] = down_gradient(routed, product, own, own - 1, range(1), spare[...]).astype(jnp.bfloat16)
+    copies[2].start()
     for copy in copies:
         copy.wait()
 
@@ -497,15 +541,24 @@
     vmem = pl.BlockSpec(memory_space=pltpu.VMEM)
     anywhere = pl.BlockSpec(memory_space=pltpu.HBM)
     dma = pltpu.SemaphoreType.DMA
-    weight_grad, gate_grad, up_grad = pl.pallas_call(
+    kept = (
+        pltpu.VMEM((own, width, hidden), half),
+        pltpu.VMEM((chunks, experts, SPLIT, cap, width), half),
+        pltpu.VMEM((n, padded, hidden), half),
+        pltpu.VMEM((n, padded, hidden), full),
+        pltpu.VMEM((n - 1, padded, hidden), half),
+        pltpu.VMEM((padded, hidden), full),
+        pltpu.VMEM((padded, hidden), full),
+        pltpu.VMEM((width, hidden), full),
+    )
+    held = sum(
+        math.prod(a.shape[:-1]) * -(-a.shape[-1] // 128) * 128 * jnp.dtype(a.dtype).itemsize for a in kept
+    )
+    parts = pl.pallas_call(
         functools.partial(kernel, (n, experts, cap, chunks, width, aligned)),
-        out_shape=(
-            pltpu.VMEM((own, width, hidden), half),
-            pltpu.VMEM((padded, hidden), half),
-            pltpu.VMEM((padded, hidden), half),
-        ),
+        out_shape=kept,
         in_specs=[anywhere] * 6,
-        out_specs=(vmem, vmem, vmem),
+        out_specs=(vmem,) * len(kept),
         scratch_shapes=[
             pltpu.VMEM(cotangent.shape, half),
             pltpu.VMEM((1, tokens), jnp.int32),
@@ -515,16 +568,10 @@
             pltpu.VMEM((own, width, hidden), half),
             dma((5 + n,)),
             pltpu.VMEM((chunks, experts, cap, width), half),
-            pltpu.VMEM((chunks, experts, SPLIT, cap, width), half),
             pltpu.VMEM((away, tokens, width), half),
             pltpu.VMEM((n - 1, 1, tokens), jnp.int32),
             pltpu.VMEM((n - 1, 1, tokens), full),
             pltpu.VMEM((n - 1, padded, hidden), half),
-            pltpu.VMEM((n - 1, padded, hidden), half),
-            pltpu.VMEM((n, padded, hidden), full),
-            pltpu.VMEM((padded, hidden), full),
-            pltpu.VMEM((padded, hidden), full),
-            pltpu.VMEM((n, padded, hidden), half),
             pltpu.VMEM((n, experts * cap, tokens), half),
             pltpu.VMEM((n, experts * cap, 1), full),
             dma((1,)),
@@ -542,7 +589,9 @@
             dma((n - 1,)),
             dma((n - 1,)),
         ],
-        compiler_params=pltpu.CompilerParams(collective_id=0, has_side_effects=True),
+        compiler_params=pltpu.CompilerParams(
+            collective_id=0, has_side_effects=True, vmem_limit_bytes=VMEM_BYTES - held
+        ),
     )(
         cotangent,
         expert_ids.reshape(1, -1),
@@ -551,15 +600,24 @@
         widen(up_pre),
         down_weight.reshape(own, width, hidden),
     )
-    results = (weight_grad.reshape(depth, hidden), gate_grad, up_grad)
     weight_grad, gate_grad, up_grad = pl.pallas_call(
-        store,
-        out_shape=[jax.ShapeDtypeStruct(a.shape, a.dtype) for a in results],
-        in_specs=[vmem] * len(results),
-        out_specs=[anywhere] * len(results),
-        scratch_shapes=[dma((len(results),))],
-        compiler_params=pltpu.CompilerParams(vmem_limit_bytes=1 << 22),
-    )(*results)
+        finish,
+        out_shape=(
+            jax.ShapeDtypeStruct((own, width, hidden), half),
+            jax.ShapeDtypeStruct((padded, hidden), half),
+            jax.ShapeDtypeStruct((padded, hidden), half),
+        ),
+        in_specs=[vmem] * len(kept),
+        out_specs=[anywhere] * 3,
+        scratch_shapes=[
+            pltpu.VMEM((width, hidden), half),
+            pltpu.VMEM((padded, hidden), half),
+            pltpu.VMEM((padded, hidden), half),
+            dma((4,)),
+        ],
+        compiler_params=pltpu.CompilerParams(vmem_limit_bytes=LAST_LIMIT),
+    )(*parts)
+    weight_grad = weight_grad.reshape(depth, hidden)
     return weight_grad, narrow(gate_grad), narrow(up_grad)
 
 

time: 44.5 us -> 44.1 us (level)
  no operation moved by 1% of the time
where the time goes in v3:
time: 44.1 us; the launch traced here: 43.9 us
  Pallas kernels  43.3 us (98%)
  between operations  0.64 us (1%)
    pallas_call x1, Pallas kernels, per_device(): pl.pallas_call(functools.partial(kernel, (n, experts, cap, chunks, width,...  42.1 us
    pallas_call x1, Pallas kernels, per_device(): pl.pallas_call(finish, out_shape=(jax.ShapeDtypeStruct((own, width, hidde...  1.21 us

profile of v3, /device:TPU:0, one launch (start us, length us, event | category | flops | bytes accessed | tf_op | source)
XLA Modules:
  0.0 43.9 jit_solution(5216557731121261731)
XLA Ops:
  0.6 42.1 %shard_map.85 = (bf16[7,256,256]{2,1,0:T(8,128)(2,1)S(1)}, bf16[14,4,4,48,256]{4,3,2,1,0:T(8,128)(2,1)S(1)}, bf16[2,768,256]{2,1,0:T(8,128)(2,1)S(1)}, f32[2,768...) custom-call(bf16[128,3584]{1,0:T(8,128)(2,1)} %cot_hbm.1, ...), custom_call_target="tpu_custom_call" | custom-call | tf_op jit(solution)/shard_map/pallas_call | solution.py:557
  42.7 1.2 %shard_map.86 = (bf16[7,256,256]{2,1,0:T(8,128)(2,1)}, bf16[768,256]{1,0:T(8,128)(2,1)}, bf16[768,256]{1,0:T(8,128)(2,1)}) custom-call(bf16[7,256,256]{2,1,0:T(8,128)(2,1)S(1)} %get-tuple-element.14.wgrad_ref, bf16[14,4,4,48,256]{4,3,2,1,0:T(8,128)(2,1)S(1)} %get-tuple-element.15.routed, bf16[2,768,256]{2,1,0:T(8,128)(2,1)S(1)} %get-tuple-element.16.product, ...), custom_call_target="tpu_custom_call" | custom-call | tf_op jit(solution)/shard_map/pallas_call | solution.py:603

commit v4 on v3

--- a/solution.py
+++ b/solution.py
@@ -12,6 +12,7 @@
 EARLY = 2
 BUILD = 3
 LAG = 2
+RING = 7
 VMEM_BYTES = 66400000
 LAST_LIMIT = 12 << 20
 
@@ -80,6 +81,7 @@
     lane_across = (lane + 2) % SPLIT
     paired = experts & (experts - 1) == 0
     steps = sorted(range(1, experts), key=lambda k: -(k.bit_length()))
+    ring = min(RING, chunks)
 
     def partner(k):
         if not paired:
@@ -214,31 +216,35 @@
     def to_beside(at, arrived):
         send(at, at, c_send.at[0], arrived, {"expert": beside}).start()
 
-    def forward_across(q):
-        all_of(routed.at[q, pl.ds(0, experts - 1), 0], y_recv.at[q])
+    def forward_across(t):
+        q = chunk_at(t)
+        all_of(routed.at[q, pl.ds(0, experts - 1), 0], y_recv.at[t % ring])
         for k in steps:
-            to_beside(routed.at[q, origin(k), lane_across], c_recv.at[q])
-
-    def to_plane(source, to, k, arrived):
-        send(source, to, z_send.at[0], arrived, {"expert": partner(k) * SPLIT + lane}).start()
+            to_beside(routed.at[q, origin(k), lane_across], c_recv.at[t % ring])
+
+    def to_plane(source, to, there, arrived):
+        send(source, to, z_send.at[0], arrived, {"expert": there * SPLIT + lane}).start()
+
+    def z_arrived(t, i):
+        return z_recv.at[jnp.where(t == final, ring + i - 1, t % ring)] if i else z_recv.at[t % ring]
 
     def to_expert(t):
         q = chunk_at(t)
         for i, k in enumerate(steps):
-            arrived = z_recv.at[t + (jnp.where(t == final, i, 0) if i else 0)]
-            to_plane(sendbuf.at[q, partner(k)], routed.at[q, e, lane], k, arrived)
+            there = partner(k)
+            to_plane(sendbuf.at[q, there], routed.at[q, e, lane], there, z_arrived(t, i))
 
         @pl.when(q >= own)
         def _():
-            to_across(q, e, y_recv.at[chunks + 1])
+            to_across(q, e, y_recv.at[ring + 1])
 
     def all_of(ref_at, sem):
         pltpu.make_async_copy(ref_at, ref_at, sem).wait()
 
-    def forward(q, k):
-        plane = origin(k)
-        to_across(q, plane, y_recv.at[q])
-        to_beside(routed.at[q, plane, lane], c_recv.at[q])
+    def forward(t, k):
+        q, plane = chunk_at(t), origin(k)
+        to_across(q, plane, y_recv.at[t % ring])
+        to_beside(routed.at[q, plane, lane], c_recv.at[t % ring])
 
     loads[0].wait()
     loads[1].wait()
@@ -262,7 +268,7 @@
     for copy in loads[3:]:
         copy.start()
     for j in range(early):
-        to_across(j, e, y_recv.at[chunks])
+        to_across(j, e, y_recv.at[ring])
 
     @pl.loop(early, own)
     def _(j):
@@ -288,9 +294,9 @@
 
     @pl.loop(early, own)
     def _(j):
-        to_across(j, e, y_recv.at[chunks])
-
-    to_beside(routed.at[pl.ds(0, own), e, lane], c_recv.at[chunks])
+        to_across(j, e, y_recv.at[ring])
+
+    to_beside(routed.at[pl.ds(0, own), e, lane], c_recv.at[ring])
 
     for k in range(1, n):
         ids_copy(k).wait_recv()
@@ -314,9 +320,9 @@
 
         @pl.when(turn == 0)
         def _():
-            all_of(routed.at[pl.ds(0, own), 0, pl.ds(0, 2)], c_recv.at[chunks])
-
-        all_of(routed.at[q, pl.ds(0, experts - 1), pl.ds(0, 2)], c_recv.at[q])
+            all_of(routed.at[pl.ds(0, own), 0, pl.ds(0, 2)], c_recv.at[ring])
+
+        all_of(routed.at[q, pl.ds(0, experts - 1), pl.ds(0, 2)], c_recv.at[turn % ring])
 
         @pl.when(k == 0)
         def _():
@@ -358,23 +364,22 @@
         def _():
             @pl.when(t == LAG)
             def _():
-                all_of(routed.at[pl.ds(0, own), 0, 0], y_recv.at[chunks])
-                to_beside(routed.at[pl.ds(0, own), e, lane_across], c_recv.at[chunks])
-
-            forward_across(chunk_at(t - LAG))
+                all_of(routed.at[pl.ds(0, own), 0, 0], y_recv.at[ring])
+                to_beside(routed.at[pl.ds(0, own), e, lane_across], c_recv.at[ring])
+
+            forward_across(t - LAG)
 
         @pl.when(t < final)
         def _():
-            q = chunk_at(t)
-            all_of(routed.at[q, pl.ds(0, experts - 1), 0], z_recv.at[t])
+            all_of(routed.at[0, pl.ds(0, experts - 1), 0], z_recv.at[t % ring])
             for k in steps:
-                forward(q, k)
+                forward(t, k)
 
         @pl.when(t == final)
         def _():
             for i, k in enumerate(steps):
-                all_of(routed.at[own - 1, 0, 0], z_recv.at[final + i])
-                forward(own - 1, k)
+                all_of(routed.at[own - 1, 0, 0], z_arrived(final, i))
+                forward(final, k)
 
         @pl.when(t + ahead < early + away)
         def _():
@@ -383,13 +388,13 @@
         @pl.when(t == home_turn)
         def _():
             theirs = pl.ds(own, away)
-            to_beside(routed.at[theirs, e, lane], c_recv.at[chunks + 1])
-            all_of(routed.at[theirs, 0, 0], y_recv.at[chunks + 1])
-            to_beside(routed.at[theirs, e, lane_across], c_recv.at[chunks + 1])
+            to_beside(routed.at[theirs, e, lane], c_recv.at[ring + 1])
+            all_of(routed.at[theirs, 0, 0], y_recv.at[ring + 1])
+            to_beside(routed.at[theirs, e, lane_across], c_recv.at[ring + 1])
 
         @pl.when(t == home_turn + 1)
         def _():
-            all_of(routed.at[pl.ds(own, away), 0, pl.ds(0, 2)], c_recv.at[chunks + 1])
+            all_of(routed.at[pl.ds(own, away), 0, pl.ds(0, 2)], c_recv.at[ring + 1])
             at = pl.ds(pl.multiple_of(e * block, 16), block)
             for k in range(1, n):
                 total = jnp.zeros((block, product.shape[2]), jnp.float32)
@@ -417,7 +422,7 @@
         def _():
             to_expert(t + ahead)
 
-    forward_across(own - 1)
+    forward_across(final)
     if rush + 1 >= steady:
         early_gradients()
 
@@ -575,11 +580,11 @@
             pltpu.VMEM((n, experts * cap, tokens), half),
             pltpu.VMEM((n, experts * cap, 1), full),
             dma((1,)),
-            dma((chunks + experts - 2,)),
+            dma((min(RING, chunks) + experts - 2,)),
             dma((1,)),
-            dma((chunks + 2,)),
+            dma((min(RING, chunks) + 2,)),
             dma((1,)),
-            dma((chunks + 2,)),
+            dma((min(RING, chunks) + 2,)),
             dma((1,)),
             dma((away,)),
             dma((n - 1, 2)),

time: 44.1 us -> 43.9 us (level)
  no operation moved by 1% of the time
where the time goes in v4:
time: 43.9 us; the launch traced here: 43.8 us
  Pallas kernels  43.1 us (98%)
  between operations  0.64 us (1%)
    pallas_call x1, Pallas kernels, per_device(): pl.pallas_call(functools.partial(kernel, (n, experts, cap, chunks, width,...  41.9 us
    pallas_call x1, Pallas kernels, per_device(): pl.pallas_call(finish, out_shape=(jax.ShapeDtypeStruct((own, width, hidde...  1.21 us

profile of v4, /device:TPU:0, one launch (start us, length us, event | category | flops | bytes accessed | tf_op | source)
XLA Modules:
  0.0 43.8 jit_solution(396873616314353985)
XLA Ops:
  0.6 41.9 %shard_map.85 = (bf16[7,256,256]{2,1,0:T(8,128)(2,1)S(1)}, bf16[14,4,4,48,256]{4,3,2,1,0:T(8,128)(2,1)S(1)}, bf16[2,768,256]{2,1,0:T(8,128)(2,1)S(1)}, f32[2,768...) custom-call(bf16[128,3584]{1,0:T(8,128)(2,1)} %cot_hbm.1, ...), custom_call_target="tpu_custom_call" | custom-call | tf_op jit(solution)/shard_map/pallas_call | solution.py:562
  42.5 1.2 %shard_map.86 = (bf16[7,256,256]{2,1,0:T(8,128)(2,1)}, bf16[768,256]{1,0:T(8,128)(2,1)}, bf16[768,256]{1,0:T(8,128)(2,1)}) custom-call(bf16[7,256,256]{2,1,0:T(8,128)(2,1)S(1)} %get-tuple-element.14.wgrad_ref, bf16[14,4,4,48,256]{4,3,2,1,0:T(8,128)(2,1)S(1)} %get-tuple-element.15.routed, bf16[2,768,256]{2,1,0:T(8,128)(2,1)S(1)} %get-tuple-element.16.product, ...), custom_call_target="tpu_custom_call" | custom-call | tf_op jit(solution)/shard_map/pallas_call | solution.py:608

commit v5 on v4

--- a/solution.py
+++ b/solution.py
@@ -12,7 +12,7 @@
 EARLY = 2
 BUILD = 3
 LAG = 2
-RING = 7
+RING = 6
 VMEM_BYTES = 66400000
 LAST_LIMIT = 12 << 20
 
@@ -310,6 +310,8 @@
     for t in range(early, ahead):
         to_expert(t)
 
+    edge = (e == 0) | (e == experts - 1)
+
     def gradient(j):
         total = jnp.zeros((width, product.shape[2]), jnp.float32)
         wgrad_ref[j] = down_gradient(routed, product, own, j, range(n), total).astype(jnp.bfloat16)
@@ -368,6 +370,10 @@
                 to_beside(routed.at[pl.ds(0, own), e, lane_across], c_recv.at[ring])
 
             forward_across(t - LAG)
+
+        @pl.when(edge & (t >= 1) & (t + ahead - 1 >= early + away) & (t + ahead - 1 < chunks))
+        def _():
+            to_expert(t + ahead - 1)
 
         @pl.when(t < final)
         def _():
@@ -418,7 +424,7 @@
             for k in range(1, n):
                 up_copy(k - 1, e).start()
 
-        @pl.when(t + ahead < chunks)
+        @pl.when((t + ahead < early + away) | ((t + ahead < chunks) & jnp.logical_not(edge)))
         def _():
             to_expert(t + ahead)
 

time: 43.9 us -> 43.9 us (level)
  no operation moved by 1% of the time
where the time goes in v5:
time: 43.9 us; the launch traced here: 43.8 us
  Pallas kernels  43.1 us (98%)
  between operations  0.64 us (1%)
    pallas_call x1, Pallas kernels, per_device(): pl.pallas_call(functools.partial(kernel, (n, experts, cap, chunks, width,...  41.9 us
    pallas_call x1, Pallas kernels, per_device(): pl.pallas_call(finish, out_shape=(jax.ShapeDtypeStruct((own, width, hidde...  1.21 us

profile of v5, /device:TPU:0, one launch (start us, length us, event | category | flops | bytes accessed | tf_op | source)
XLA Modules:
  0.0 43.8 jit_solution(5598851444391811395)
XLA Ops:
  0.6 41.9 %shard_map.85 = (bf16[7,256,256]{2,1,0:T(8,128)(2,1)S(1)}, bf16[14,4,4,48,256]{4,3,2,1,0:T(8,128)(2,1)S(1)}, bf16[2,768,256]{2,1,0:T(8,128)(2,1)S(1)}, f32[2,768...) custom-call(bf16[128,3584]{1,0:T(8,128)(2,1)} %cot_hbm.1, ...), custom_call_target="tpu_custom_call" | custom-call | tf_op jit(solution)/shard_map/pallas_call | solution.py:568
  42.6 1.2 %shard_map.86 = (bf16[7,256,256]{2,1,0:T(8,128)(2,1)}, bf16[768,256]{1,0:T(8,128)(2,1)}, bf16[768,256]{1,0:T(8,128)(2,1)}) custom-call(bf16[7,256,256]{2,1,0:T(8,128)(2,1)S(1)} %get-tuple-element.14.wgrad_ref, bf16[14,4,4,48,256]{4,3,2,1,0:T(8,128)(2,1)S(1)} %get-tuple-element.15.routed, bf16[2,768,256]{2,1,0:T(8,128)(2,1)S(1)} %get-tuple-element.16.product, ...), custom_call_target="tpu_custom_call" | custom-call | tf_op jit(solution)/shard_map/pallas_call | solution.py:614
